TPU v7x, 32 devices: a whole 2x2x4 slice. The times are simulated.
32 devices in a mesh: gene: 8 (over z, x), cell: 4 (over y, core).
Axes of the slice: x: 2, y: 2, z: 4, core: 2. Of those that a mesh axis runs over, the one named last changes fastest.
Arguments:
- pool_counts: bfloat16 [20480, 16384], P('gene', 'cell'), may hold values from 0 to 6.5
- cell_picks: int32 [7, 4096], P(None, 'cell'), may hold values from 0 to 16383, as said below
- loadings_init: float32 [64, 20480], P(None, 'gene'), may hold values from -0.0390625 to 0.0390625
Outputs:
- scaled_loadings: float32 [64, 20480], P(None, 'gene')
Inputs may be any that keep to these rules, and one draw needn't show every extreme that they name: `cell_picks`: column b of every row names a pool cell in [(b // 1024) * 4096, (b // 1024 + 1) * 4096); no cell is named twice in one row.
All inputs are finite; a program needn't handle non-finite values.
Results may differ from a plain program's by a relative error of at most 0.018.
Values may be sent and summed in bfloat16 or wider, within the bound.
A program may use at most 128 MiB of HBM per device.

v0:
```python
import math
import jax
import jax.numpy as jnp
from jax import lax
from jax.sharding import PartitionSpec as P

STEPS = 7
step_rate = 1.0


def transposed_product(left, right):
    return lax.dot_general(
        left, right, (((1,), (1,)), ((), ())), preferred_element_type=jnp.float32
    )


def shards(pool_counts, cell_picks, loadings_init):
    loadings = loadings_init
    local_pool = pool_counts.shape[1]
    group = lax.axis_index("cell")
    batch_total = cell_picks.shape[1] * lax.axis_size("cell")
    gene_total = loadings.shape[1] * lax.axis_size("gene")
    for step_index in range(STEPS):
        chosen = cell_picks[step_index] - group * local_pool
        gathered = jnp.take(pool_counts, chosen, axis=1)
        weights_low = loadings.astype(jnp.bfloat16)
        product = jnp.dot(weights_low, gathered, preferred_element_type=jnp.float32)
        local_sums = jnp.sum(gathered, axis=1, dtype=jnp.float32)
        batch_means = lax.psum(local_sums, "cell") / batch_total
        shift = jnp.dot(
            weights_low.astype(jnp.float32), batch_means, precision=lax.Precision.HIGHEST
        )
        partial_value = product - shift[:, None]
        scores = lax.psum(partial_value, "gene")
        scores_low = scores.astype(jnp.bfloat16)
        raw_update = transposed_product(scores_low, gathered)
        row_totals = jnp.sum(scores_low, axis=1, dtype=jnp.float32)
        local_update = (raw_update - row_totals[:, None] * batch_means[None, :]) / batch_total
        update = lax.psum(local_update.astype(jnp.bfloat16), "cell").astype(jnp.float32)
        stepped = loadings + step_rate * update
        gram_part = jnp.dot(stepped, stepped.T, precision=lax.Precision.HIGHEST)
        gram_matrix = lax.psum(gram_part, "gene")
        factor = jnp.linalg.cholesky(gram_matrix)
        loadings = lax.linalg.triangular_solve(factor, stepped, left_side=True, lower=True)
    return loadings * math.sqrt(gene_total)


def solution(mesh):
    placed = (P("gene", "cell"), P(None, "cell"), P(None, "gene"))
    return jax.shard_map(
        shards, mesh=mesh, in_specs=placed, out_specs=P(None, "gene"), check_vma=False
    )
```

profile of v0, /device:TPU:0, one launch (start us, length us, event | category | flops | bytes accessed | tf_op | source)
XLA Modules:
  0.0 1143.4 jit_solution(7488319310404820462)
XLA Ops:
  7.8 25.9 %copy.4 = bf16[2560,4096]{0,1:T(8,128)(2,1)} copy(bf16[2560,4096]{1,0:T(8,128)(2,1)} %param.8) | data formatting | bytes 41943040 | tf_op args[0]
  73.9 20.5 %gather_fusion.4 = bf16[1024,2560]{1,0:T(8,128)(2,1)} fusion(bf16[2560,4096]{0,1:T(8,128)(2,1)} %copy.4, s32[1024]{0:T(1024)S(1)} %fusion.186), kind=kCustom, calls=%fused_computation.4.clone | custom fusion | bytes 10489856 | tf_op jit(solution)/shard_map/jit(_take)/gather | solution.py:25
  195.6 33.5 %all-reduce.31.cloned.1.call-done = (f32[2560]{0:T(1024)}, f32[2560]{0:T(1024)}, f32[2560]{0:T(1024)}, f32[2560]{0:T(1024)}, f32[2560]{0:T(1024)}, /*index=5*/f32[2560]{0:T(1024)}, f32[2560]{0:T(1024)}) async-done(((f32[2560]{0:T(1024)}, f32[2560]{0:T(1024)}, f32[2560]{0:T(1024)}, f32[2560]{0:T(1024)}, f32[2560]{0:T(1024)}, /*index=5*/f32[2560]{0:T(1024)}, f32[2560]{0:T(1024)}), (f32[2560]{0:T(1024)}, ...) | async-done | bytes 71696 | tf_op jit(solution)/shard_map/psum | solution.py:29
  234.5 40.8 %all-reduce.32 = bf16[64,1024]{1,0:T(8,128)(2,1)S(1)} all-reduce(f32[64,1024]{1,0:T(8,128)S(1)} %fusion.94), channel_id=1, replica_groups=mesh['gene'=8,'cell'=4] {'gene'}, use_global_device_ids=true, to_apply=%region_2.4 | all-reduce | flops 65536 | bytes 393216 | tf_op jit(solution)/shard_map/psum | solution.py:34
  279.9 30.0 %all-reduce.17.cloned.1.call-done = bf16[64,2560]{1,0:T(8,128)(2,1)} async-done(((bf16[64,2560]{1,0:T(8,128)(2,1)}), bf16[64,2560]{1,0:T(8,128)(2,1)}) %all-reduce.17.cloned.1.call-update) | async-done | bytes 327696 | tf_op jit(solution)/shard_map/psum | solution.py:39
  311.8 37.1 %psum.199 = f32[64,64]{0,1:T(8,128)S(1)} all-reduce(f32[64,64]{0,1:T(8,128)S(1)} %fusion.116), channel_id=1, replica_groups=mesh['gene'=8,'cell'=4] {'gene'}, use_global_device_ids=true, to_apply=%region_5.7 | all-reduce | flops 4096 | bytes 32768 | tf_op jit(solution)/shard_map/psum | solution.py:42
  367.4 36.0 %all-reduce.33 = bf16[64,1024]{1,0:T(8,128)(2,1)S(1)} all-reduce(f32[64,1024]{1,0:T(8,128)S(1)} %fusion.97), channel_id=1, replica_groups=mesh['gene'=8,'cell'=4] {'gene'}, use_global_device_ids=true, to_apply=%region_10.0 | all-reduce | flops 65536 | bytes 393216 | tf_op jit(solution)/shard_map/psum | solution.py:34
  408.1 30.5 %all-reduce.19.cloned.1.call-done = bf16[64,2560]{1,0:T(8,128)(2,1)} async-done(((bf16[64,2560]{1,0:T(8,128)(2,1)}), bf16[64,2560]{1,0:T(8,128)(2,1)}) %all-reduce.19.cloned.1.call-update) | async-done | bytes 327696 | tf_op jit(solution)/shard_map/psum | solution.py:39
  440.4 37.6 %psum.203 = f32[64,64]{0,1:T(8,128)S(1)} all-reduce(f32[64,64]{0,1:T(8,128)S(1)} %fusion.118), channel_id=1, replica_groups=mesh['gene'=8,'cell'=4] {'gene'}, use_global_device_ids=true, to_apply=%region_13.0 | all-reduce | flops 4096 | bytes 32768 | tf_op jit(solution)/shard_map/psum | solution.py:42
  496.6 36.0 %all-reduce.34 = bf16[64,1024]{1,0:T(8,128)(2,1)S(1)} all-reduce(f32[64,1024]{1,0:T(8,128)S(1)} %fusion.100), channel_id=1, replica_groups=mesh['gene'=8,'cell'=4] {'gene'}, use_global_device_ids=true, to_apply=%region_16.0 | all-reduce | flops 65536 | bytes 393216 | tf_op jit(solution)/shard_map/psum | solution.py:34
  537.2 30.6 %all-reduce.21.cloned.1.call-done = bf16[64,2560]{1,0:T(8,128)(2,1)} async-done(((bf16[64,2560]{1,0:T(8,128)(2,1)}), bf16[64,2560]{1,0:T(8,128)(2,1)}) %all-reduce.21.cloned.1.call-update) | async-done | bytes 327696 | tf_op jit(solution)/shard_map/psum | solution.py:39
  569.7 37.1 %psum.207 = f32[64,64]{0,1:T(8,128)S(1)} all-reduce(f32[64,64]{0,1:T(8,128)S(1)} %fusion.120), channel_id=1, replica_groups=mesh['gene'=8,'cell'=4] {'gene'}, use_global_device_ids=true, to_apply=%region_19.0 | all-reduce | flops 4096 | bytes 32768 | tf_op jit(solution)/shard_map/psum | solution.py:42
  625.3 36.0 %all-reduce.35 = bf16[64,1024]{1,0:T(8,128)(2,1)S(1)} all-reduce(f32[64,1024]{1,0:T(8,128)S(1)} %fusion.103), channel_id=1, replica_groups=mesh['gene'=8,'cell'=4] {'gene'}, use_global_device_ids=true, to_apply=%region_22.0 | all-reduce | flops 65536 | bytes 393216 | tf_op jit(solution)/shard_map/psum | solution.py:34
  666.2 30.4 %all-reduce.23.cloned.1.call-done = bf16[64,2560]{1,0:T(8,128)(2,1)} async-done(((bf16[64,2560]{1,0:T(8,128)(2,1)}), bf16[64,2560]{1,0:T(8,128)(2,1)}) %all-reduce.23.cloned.1.call-update) | async-done | bytes 327696 | tf_op jit(solution)/shard_map/psum | solution.py:39
  698.4 37.1 %psum.211 = f32[64,64]{0,1:T(8,128)S(1)} all-reduce(f32[64,64]{0,1:T(8,128)S(1)} %fusion.122), channel_id=1, replica_groups=mesh['gene'=8,'cell'=4] {'gene'}, use_global_device_ids=true, to_apply=%region_25.0 | all-reduce | flops 4096 | bytes 32768 | tf_op jit(solution)/shard_map/psum | solution.py:42
  754.0 36.0 %all-reduce.36 = bf16[64,1024]{1,0:T(8,128)(2,1)S(1)} all-reduce(f32[64,1024]{1,0:T(8,128)S(1)} %fusion.106), channel_id=1, replica_groups=mesh['gene'=8,'cell'=4] {'gene'}, use_global_device_ids=true, to_apply=%region_28.0 | all-reduce | flops 65536 | bytes 393216 | tf_op jit(solution)/shard_map/psum | solution.py:34
  794.6 30.7 %all-reduce.25.cloned.1.call-done = bf16[64,2560]{1,0:T(8,128)(2,1)} async-done(((bf16[64,2560]{1,0:T(8,128)(2,1)}), bf16[64,2560]{1,0:T(8,128)(2,1)}) %all-reduce.25.cloned.1.call-update) | async-done | bytes 327696 | tf_op jit(solution)/shard_map/psum | solution.py:39
  827.1 37.1 %psum.215 = f32[64,64]{0,1:T(8,128)S(1)} all-reduce(f32[64,64]{0,1:T(8,128)S(1)} %fusion.124), channel_id=1, replica_groups=mesh['gene'=8,'cell'=4] {'gene'}, use_global_device_ids=true, to_apply=%region_31.0 | all-reduce | flops 4096 | bytes 32768 | tf_op jit(solution)/shard_map/psum | solution.py:42
  882.8 36.2 %all-reduce.37 = bf16[64,1024]{1,0:T(8,128)(2,1)S(1)} all-reduce(f32[64,1024]{1,0:T(8,128)S(1)} %fusion.109), channel_id=1, replica_groups=mesh['gene'=8,'cell'=4] {'gene'}, use_global_device_ids=true, to_apply=%region_34.0 | all-reduce | flops 65536 | bytes 393216 | tf_op jit(solution)/shard_map/psum | solution.py:34
  923.6 30.5 %all-reduce.27.cloned.1.call-done = bf16[64,2560]{1,0:T(8,128)(2,1)} async-done(((bf16[64,2560]{1,0:T(8,128)(2,1)}), bf16[64,2560]{1,0:T(8,128)(2,1)}) %all-reduce.27.cloned.1.call-update) | async-done | bytes 327696 | tf_op jit(solution)/shard_map/psum | solution.py:39
  956.0 37.1 %psum.219 = f32[64,64]{0,1:T(8,128)S(1)} all-reduce(f32[64,64]{0,1:T(8,128)S(1)} %fusion.126), channel_id=1, replica_groups=mesh['gene'=8,'cell'=4] {'gene'}, use_global_device_ids=true, to_apply=%region_37.0 | all-reduce | flops 4096 | bytes 32768 | tf_op jit(solution)/shard_map/psum | solution.py:42
  1011.6 35.9 %all-reduce.38 = bf16[64,1024]{1,0:T(8,128)(2,1)S(1)} all-reduce(f32[64,1024]{1,0:T(8,128)S(1)} %fusion.112), channel_id=1, replica_groups=mesh['gene'=8,'cell'=4] {'gene'}, use_global_device_ids=true, to_apply=%region_40.0 | all-reduce | flops 65536 | bytes 393216 | tf_op jit(solution)/shard_map/psum | solution.py:34
  1052.1 30.7 %all-reduce.29.cloned.1.call-done = bf16[64,2560]{1,0:T(8,128)(2,1)} async-done(((bf16[64,2560]{1,0:T(8,128)(2,1)}), bf16[64,2560]{1,0:T(8,128)(2,1)}) %all-reduce.29.cloned.1.call-update) | async-done | bytes 327696 | tf_op jit(solution)/shard_map/psum | solution.py:39
  1084.5 37.1 %psum.223 = f32[64,64]{0,1:T(8,128)S(1)} all-reduce(f32[64,64]{0,1:T(8,128)S(1)} %fusion.127), channel_id=1, replica_groups=mesh['gene'=8,'cell'=4] {'gene'}, use_global_device_ids=true, to_apply=%region_43.47 | all-reduce | flops 4096 | bytes 32768 | tf_op jit(solution)/shard_map/psum | solution.py:42
  (175 shorter events, 318.5 us)
Async XLA Ops:
  6.5 222.6 %all-reduce.31.cloned.1.call-start = ((), (), s32[]{:S(2)}) async-start(), calls=%async_computation.7 | async-start | bytes 172032 | tf_op jit(solution)/shard_map/psum | solution.py:29
  175.0 11.6 %slice-start = ((s8[5242880]{0:T(1024)(128)(4,1)}), s8[1048576]{0:T(1024)(128)(4,1)S(1)}, s32[]{:S(2)}) async-start(s8[5242880]{0:T(1024)(128)(4,1)} %bitcast.200), calls=%async_computation.8 | async-start | bytes 2097152
  179.3 7.3 slice-start.1
  179.3 12.7 %slice-start.2 = ((s8[5242880]{0:T(1024)(128)(4,1)}), s8[4194304]{0:T(1024)(128)(4,1)S(1)}, s32[]{:S(2)}) async-start(s8[5242880]{0:T(1024)(128)(4,1)} %bitcast.202), calls=%async_computation.10 | async-start | bytes 8388608
  179.3 12.7 %slice-start.4 = ((s8[5242880]{0:T(1024)(128)(4,1)}), s8[4194304]{0:T(1024)(128)(4,1)S(1)}, s32[]{:S(2)}) async-start(s8[5242880]{0:T(1024)(128)(4,1)} %bitcast.204), calls=%async_computation.12 | async-start | bytes 8388608
  186.6 5.4 slice-start.3
  186.6 5.4 slice-start.5
  192.0 37.8 %copy-start = (f32[64,2560]{1,0:T(8,128)S(1)}, f32[64,2560]{1,0:T(8,128)}, u32[]{:S(2)}) copy-start(f32[64,2560]{1,0:T(8,128)} %param.10) | copy-start | bytes 1966084
  195.6 114.4 %all-reduce.17.cloned.1.call-start = ((), (), s32[]{:S(2)}) async-start(), calls=%async_computation | async-start | bytes 655360 | tf_op jit(solution)/shard_map/psum | solution.py:39
  234.5 45.4 %copy-start.6 = (f32[2560]{0:T(1024)S(1)}, f32[2560]{0:T(1024)}, u32[]{:S(2)}) copy-start(f32[2560]{0:T(1024)} %get-tuple-element.8) | copy-start | bytes 30724
  279.8 158.7 %all-reduce.19.cloned.1.call-start = ((), (), s32[]{:S(2)}) async-start(), calls=%async_computation.1 | async-start | bytes 655360 | tf_op jit(solution)/shard_map/psum | solution.py:39
  367.4 40.6 %copy-start.5 = (f32[2560]{0:T(1024)S(1)}, f32[2560]{0:T(1024)}, u32[]{:S(2)}) copy-start(f32[2560]{0:T(1024)} %get-tuple-element.10) | copy-start | bytes 30724
  408.0 159.9 %all-reduce.21.cloned.1.call-start = ((), (), s32[]{:S(2)}) async-start(), calls=%async_computation.2 | async-start | bytes 655360 | tf_op jit(solution)/shard_map/psum | solution.py:39
  496.6 40.6 %copy-start.4 = (f32[2560]{0:T(1024)S(1)}, f32[2560]{0:T(1024)}, u32[]{:S(2)}) copy-start(f32[2560]{0:T(1024)} %get-tuple-element.11) | copy-start | bytes 30724
  537.1 159.4 %all-reduce.23.cloned.1.call-start = ((), (), s32[]{:S(2)}) async-start(), calls=%async_computation.3 | async-start | bytes 655360 | tf_op jit(solution)/shard_map/psum | solution.py:39
  625.3 40.8 %copy-start.3 = (f32[2560]{0:T(1024)S(1)}, f32[2560]{0:T(1024)}, u32[]{:S(2)}) copy-start(f32[2560]{0:T(1024)} %get-tuple-element.12) | copy-start | bytes 30724
  665.9 159.4 %all-reduce.25.cloned.1.call-start = ((), (), s32[]{:S(2)}) async-start(), calls=%async_computation.4 | async-start | bytes 655360 | tf_op jit(solution)/shard_map/psum | solution.py:39
  754.0 40.6 %copy-start.2 = (f32[2560]{0:T(1024)S(1)}, f32[2560]{0:T(1024)}, u32[]{:S(2)}) copy-start(f32[2560]{0:T(1024)} %get-tuple-element.13) | copy-start | bytes 30724
  794.5 159.6 %all-reduce.27.cloned.1.call-start = ((), (), s32[]{:S(2)}) async-start(), calls=%async_computation.5 | async-start | bytes 655360 | tf_op jit(solution)/shard_map/psum | solution.py:39
  882.8 40.9 %copy-start.1 = (f32[2560]{0:T(1024)S(1)}, f32[2560]{0:T(1024)}, u32[]{:S(2)}) copy-start(f32[2560]{0:T(1024)} %get-tuple-element.14) | copy-start | bytes 30724
  923.5 159.2 %all-reduce.29.cloned.1.call-start = ((), (), s32[]{:S(2)}) async-start(), calls=%async_computation.6 | async-start | bytes 655360 | tf_op jit(solution)/shard_map/psum | solution.py:39
Sparse Core Ops, SparseCore 0:
  195.7 33.3 all-reduce.30
  280.0 29.9 all-reduce.16
  408.1 30.4 all-reduce.18
  537.3 30.5 all-reduce.20
  666.0 30.5 all-reduce.22
  794.7 30.5 all-reduce.24
  923.7 30.4 all-reduce.26
  1052.2 30.4 all-reduce.28
where the time goes:
time: 1150 us; the launch traced here: 1140 us
  blocking collectives  517 us (45%)
  waiting for transfers between devices  247 us (21%)
  local copies, waits for them, and re-layouts  168 us (15%)
  other arithmetic  108 us (9%)
  matrix products  88.8 us (8%)
  between operations  14.4 us (1%)
    psum x7, blocking collectives, shards(): gram_matrix = lax.psum(gram_part, 'gene')  260 us
    psum x7, blocking collectives, shards(): scores = lax.psum(partial_value, 'gene')  257 us
    psum x7, waiting for transfers between devices, shards(): lax.psum(local_update.astype(jnp.bfloat16), 'cell').astype(jnp.float32)  213 us
    gather x7, local copies, waits for them, and re-layouts, shards(): gathered = jnp.take(pool_counts, chosen, axis=1)  141 us
    another operation x21, other arithmetic, shards(): factor = jnp.linalg.cholesky(gram_matrix)  45.6 us
    another operation x14, other arithmetic, shards(): lax.linalg.triangular_solve(factor, stepped, left_side=True, lower=True)  38.8 us
    psum x1, waiting for transfers between devices, shards(): batch_means = lax.psum(local_sums, 'cell') / batch_total  33.5 us
    dot_general x7, matrix products, transposed_product(): lax.dot_general(left, right, (((1,), (1,)), ((), ())), preferred_element_...  30.7 us
  transfers between devices with their start and end apart: 8, of which 8 were waited for; matrix products, arithmetic and copies ran while one was open for 0% of the time, Pallas kernels for 0%

commit v1 on v0

--- a/solution.py
+++ b/solution.py
@@ -39,7 +39,8 @@
         update = lax.psum(local_update.astype(jnp.bfloat16), "cell").astype(jnp.float32)
         stepped = loadings + step_rate * update
         gram_part = jnp.dot(stepped, stepped.T, precision=lax.Precision.HIGHEST)
-        gram_matrix = lax.psum(gram_part, "gene")
+        blocks = lax.all_gather(gram_part, "gene", axis=0, tiled=False)
+        gram_matrix = blocks.sum(axis=0)
         factor = jnp.linalg.cholesky(gram_matrix)
         loadings = lax.linalg.triangular_solve(factor, stepped, left_side=True, lower=True)
     return loadings * math.sqrt(gene_total)

time: 1150 us -> 1130 us (0.983)
  blocking collectives: 517 us -> 498 us
    psum x7 -> x0, blocking collectives: 260 us -> none  [shards(): gram_matrix = lax.psum(gram_part, 'gene')]
    all_gather x0 -> x7, blocking collectives: none -> 217 us  [shards(): blocks = lax.all_gather(gram_part, 'gene', axis=0, tiled=False)]
    psum x7, blocking collectives: 257 us -> 281 us  [shards(): scores = lax.psum(partial_value, 'gene')]
where the time goes in v1:
time: 1130 us; the launch traced here: 1120 us
  blocking collectives  498 us (44%)
  waiting for transfers between devices  237 us (21%)
  local copies, waits for them, and re-layouts  168 us (15%)
  other arithmetic  108 us (10%)
  matrix products  88.8 us (8%)
  between operations  14.4 us (1%)
    psum x7, blocking collectives, shards(): scores = lax.psum(partial_value, 'gene')  281 us
    all_gather x7, blocking collectives, shards(): blocks = lax.all_gather(gram_part, 'gene', axis=0, tiled=False)  217 us
    psum x7, waiting for transfers between devices, shards(): lax.psum(local_update.astype(jnp.bfloat16), 'cell').astype(jnp.float32)  204 us
    gather x7, local copies, waits for them, and re-layouts, shards(): gathered = jnp.take(pool_counts, chosen, axis=1)  141 us
    another operation x21, other arithmetic, shards(): factor = jnp.linalg.cholesky(gram_matrix)  45.6 us
    another operation x14, other arithmetic, shards(): lax.linalg.triangular_solve(factor, stepped, left_side=True, lower=True)  38.8 us
    psum x1, waiting for transfers between devices, shards(): batch_means = lax.psum(local_sums, 'cell') / batch_total  33.5 us
    dot_general x7, matrix products, transposed_product(): lax.dot_general(left, right, (((1,), (1,)), ((), ())), preferred_element_...  30.8 us
  transfers between devices with their start and end apart: 8, of which 8 were waited for; matrix products, arithmetic and copies ran while one was open for 0% of the time, Pallas kernels for 0%

profile of v1, /device:TPU:0, one launch (start us, length us, event | category | flops | bytes accessed | tf_op | source)
XLA Modules:
  0.0 1115.2 jit_solution(12930984549426212991)
XLA Ops:
  7.8 25.9 %copy.18 = bf16[2560,4096]{0,1:T(8,128)(2,1)} copy(bf16[2560,4096]{1,0:T(8,128)(2,1)} %param.8) | data formatting | bytes 41943040 | tf_op args[0]
  73.9 20.5 %gather_fusion.4 = bf16[1024,2560]{1,0:T(8,128)(2,1)} fusion(bf16[2560,4096]{0,1:T(8,128)(2,1)} %copy.18, s32[1024]{0:T(1024)S(1)} %fusion.186), kind=kCustom, calls=%fused_computation.4.clone | custom fusion | bytes 10489856 | tf_op jit(solution)/shard_map/jit(_take)/gather | solution.py:25
  195.6 33.5 %all-reduce.31.cloned.1.call-done = (f32[2560]{0:T(1024)}, f32[2560]{0:T(1024)}, f32[2560]{0:T(1024)}, f32[2560]{0:T(1024)}, f32[2560]{0:T(1024)}, /*index=5*/f32[2560]{0:T(1024)}, f32[2560]{0:T(1024)}) async-done(((f32[2560]{0:T(1024)}, f32[2560]{0:T(1024)}, f32[2560]{0:T(1024)}, f32[2560]{0:T(1024)}, f32[2560]{0:T(1024)}, /*index=5*/f32[2560]{0:T(1024)}, f32[2560]{0:T(1024)}), (f32[2560]{0:T(1024)}, ...) | async-done | bytes 71696 | tf_op jit(solution)/shard_map/psum | solution.py:29
  234.5 40.8 %all-reduce.32 = bf16[64,1024]{1,0:T(8,128)(2,1)S(1)} all-reduce(f32[64,1024]{1,0:T(8,128)S(1)} %fusion.94), channel_id=1, replica_groups=mesh['gene'=8,'cell'=4] {'gene'}, use_global_device_ids=true, to_apply=%region_2.4 | all-reduce | flops 65536 | bytes 393216 | tf_op jit(solution)/shard_map/psum | solution.py:34
  279.9 30.0 %all-reduce.17.cloned.1.call-done = bf16[64,2560]{1,0:T(8,128)(2,1)} async-done(((bf16[64,2560]{1,0:T(8,128)(2,1)}), bf16[64,2560]{1,0:T(8,128)(2,1)}) %all-reduce.17.cloned.1.call-update) | async-done | bytes 327696 | tf_op jit(solution)/shard_map/psum | solution.py:39
  311.8 30.9 %all-gather = f32[512,64]{1,0:T(8,128)S(1)} all-gather(f32[64,64]{1,0:T(8,128)S(1)} %fusion.116), channel_id=2, replica_groups=mesh['gene'=8,'cell'=4] {'gene'}, dimensions={0}, use_global_device_ids=true | all-gather | bytes 147456 | tf_op jit(solution)/shard_map/all_gather | solution.py:42
  361.3 40.1 %all-reduce.33 = bf16[64,1024]{1,0:T(8,128)(2,1)S(1)} all-reduce(f32[64,1024]{1,0:T(8,128)S(1)} %fusion.97), channel_id=1, replica_groups=mesh['gene'=8,'cell'=4] {'gene'}, use_global_device_ids=true, to_apply=%region_10.0 | all-reduce | flops 65536 | bytes 393216 | tf_op jit(solution)/shard_map/psum | solution.py:34
  406.0 29.0 %all-reduce.19.cloned.1.call-done = bf16[64,2560]{1,0:T(8,128)(2,1)} async-done(((bf16[64,2560]{1,0:T(8,128)(2,1)}), bf16[64,2560]{1,0:T(8,128)(2,1)}) %all-reduce.19.cloned.1.call-update) | async-done | bytes 327696 | tf_op jit(solution)/shard_map/psum | solution.py:39
  436.7 31.3 %all-gather.1 = f32[512,64]{1,0:T(8,128)S(1)} all-gather(f32[64,64]{1,0:T(8,128)S(1)} %fusion.118), channel_id=3, replica_groups=mesh['gene'=8,'cell'=4] {'gene'}, dimensions={0}, use_global_device_ids=true | all-gather | bytes 147456 | tf_op jit(solution)/shard_map/all_gather | solution.py:42
  486.7 40.2 %all-reduce.34 = bf16[64,1024]{1,0:T(8,128)(2,1)S(1)} all-reduce(f32[64,1024]{1,0:T(8,128)S(1)} %fusion.100), channel_id=1, replica_groups=mesh['gene'=8,'cell'=4] {'gene'}, use_global_device_ids=true, to_apply=%region_16.0 | all-reduce | flops 65536 | bytes 393216 | tf_op jit(solution)/shard_map/psum | solution.py:34
  531.5 29.0 %all-reduce.21.cloned.1.call-done = bf16[64,2560]{1,0:T(8,128)(2,1)} async-done(((bf16[64,2560]{1,0:T(8,128)(2,1)}), bf16[64,2560]{1,0:T(8,128)(2,1)}) %all-reduce.21.cloned.1.call-update) | async-done | bytes 327696 | tf_op jit(solution)/shard_map/psum | solution.py:39
  562.3 30.9 %all-gather.2 = f32[512,64]{1,0:T(8,128)S(1)} all-gather(f32[64,64]{1,0:T(8,128)S(1)} %fusion.120), channel_id=4, replica_groups=mesh['gene'=8,'cell'=4] {'gene'}, dimensions={0}, use_global_device_ids=true | all-gather | bytes 147456 | tf_op jit(solution)/shard_map/all_gather | solution.py:42
  611.8 40.1 %all-reduce.35 = bf16[64,1024]{1,0:T(8,128)(2,1)S(1)} all-reduce(f32[64,1024]{1,0:T(8,128)S(1)} %fusion.103), channel_id=1, replica_groups=mesh['gene'=8,'cell'=4] {'gene'}, use_global_device_ids=true, to_apply=%region_22.0 | all-reduce | flops 65536 | bytes 393216 | tf_op jit(solution)/shard_map/psum | solution.py:34
  656.7 28.8 %all-reduce.23.cloned.1.call-done = bf16[64,2560]{1,0:T(8,128)(2,1)} async-done(((bf16[64,2560]{1,0:T(8,128)(2,1)}), bf16[64,2560]{1,0:T(8,128)(2,1)}) %all-reduce.23.cloned.1.call-update) | async-done | bytes 327696 | tf_op jit(solution)/shard_map/psum | solution.py:39
  687.3 30.9 %all-gather.3 = f32[512,64]{1,0:T(8,128)S(1)} all-gather(f32[64,64]{1,0:T(8,128)S(1)} %fusion.122), channel_id=5, replica_groups=mesh['gene'=8,'cell'=4] {'gene'}, dimensions={0}, use_global_device_ids=true | all-gather | bytes 147456 | tf_op jit(solution)/shard_map/all_gather | solution.py:42
  736.8 40.1 %all-reduce.36 = bf16[64,1024]{1,0:T(8,128)(2,1)S(1)} all-reduce(f32[64,1024]{1,0:T(8,128)S(1)} %fusion.106), channel_id=1, replica_groups=mesh['gene'=8,'cell'=4] {'gene'}, use_global_device_ids=true, to_apply=%region_28.0 | all-reduce | flops 65536 | bytes 393216 | tf_op jit(solution)/shard_map/psum | solution.py:34
  781.5 29.0 %all-reduce.25.cloned.1.call-done = bf16[64,2560]{1,0:T(8,128)(2,1)} async-done(((bf16[64,2560]{1,0:T(8,128)(2,1)}), bf16[64,2560]{1,0:T(8,128)(2,1)}) %all-reduce.25.cloned.1.call-update) | async-done | bytes 327696 | tf_op jit(solution)/shard_map/psum | solution.py:39
  812.2 30.9 %all-gather.4 = f32[512,64]{1,0:T(8,128)S(1)} all-gather(f32[64,64]{1,0:T(8,128)S(1)} %fusion.124), channel_id=6, replica_groups=mesh['gene'=8,'cell'=4] {'gene'}, dimensions={0}, use_global_device_ids=true | all-gather | bytes 147456 | tf_op jit(solution)/shard_map/all_gather | solution.py:42
  861.8 40.3 %all-reduce.37 = bf16[64,1024]{1,0:T(8,128)(2,1)S(1)} all-reduce(f32[64,1024]{1,0:T(8,128)S(1)} %fusion.109), channel_id=1, replica_groups=mesh['gene'=8,'cell'=4] {'gene'}, use_global_device_ids=true, to_apply=%region_34.0 | all-reduce | flops 65536 | bytes 393216 | tf_op jit(solution)/shard_map/psum | solution.py:34
  906.7 29.0 %all-reduce.27.cloned.1.call-done = bf16[64,2560]{1,0:T(8,128)(2,1)} async-done(((bf16[64,2560]{1,0:T(8,128)(2,1)}), bf16[64,2560]{1,0:T(8,128)(2,1)}) %all-reduce.27.cloned.1.call-update) | async-done | bytes 327696 | tf_op jit(solution)/shard_map/psum | solution.py:39
  937.5 30.9 %all-gather.5 = f32[512,64]{1,0:T(8,128)S(1)} all-gather(f32[64,64]{1,0:T(8,128)S(1)} %fusion.126), channel_id=7, replica_groups=mesh['gene'=8,'cell'=4] {'gene'}, dimensions={0}, use_global_device_ids=true | all-gather | bytes 147456 | tf_op jit(solution)/shard_map/all_gather | solution.py:42
  987.0 40.0 %all-reduce.38 = bf16[64,1024]{1,0:T(8,128)(2,1)S(1)} all-reduce(f32[64,1024]{1,0:T(8,128)S(1)} %fusion.112), channel_id=1, replica_groups=mesh['gene'=8,'cell'=4] {'gene'}, use_global_device_ids=true, to_apply=%region_40.0 | all-reduce | flops 65536 | bytes 393216 | tf_op jit(solution)/shard_map/psum | solution.py:34
  1031.6 29.0 %all-reduce.29.cloned.1.call-done = bf16[64,2560]{1,0:T(8,128)(2,1)} async-done(((bf16[64,2560]{1,0:T(8,128)(2,1)}), bf16[64,2560]{1,0:T(8,128)(2,1)}) %all-reduce.29.cloned.1.call-update) | async-done | bytes 327696 | tf_op jit(solution)/shard_map/psum | solution.py:39
  1062.4 30.9 %all-gather.6 = f32[512,64]{1,0:T(8,128)S(1)} all-gather(f32[64,64]{1,0:T(8,128)S(1)} %fusion.127), channel_id=8, replica_groups=mesh['gene'=8,'cell'=4] {'gene'}, dimensions={0}, use_global_device_ids=true | all-gather | bytes 147456 | tf_op jit(solution)/shard_map/all_gather | solution.py:42
  (182 shorter events, 318.7 us)
Async XLA Ops:
  6.5 222.6 %all-reduce.31.cloned.1.call-start = ((), (), s32[]{:S(2)}) async-start(), calls=%async_computation.7 | async-start | bytes 172032 | tf_op jit(solution)/shard_map/psum | solution.py:29
  175.0 11.6 %slice-start = ((s8[5242880]{0:T(1024)(128)(4,1)}), s8[1048576]{0:T(1024)(128)(4,1)S(1)}, s32[]{:S(2)}) async-start(s8[5242880]{0:T(1024)(128)(4,1)} %bitcast.207), calls=%async_computation.8 | async-start | bytes 2097152
  179.3 7.3 slice-start.1
  179.3 12.7 %slice-start.2 = ((s8[5242880]{0:T(1024)(128)(4,1)}), s8[4194304]{0:T(1024)(128)(4,1)S(1)}, s32[]{:S(2)}) async-start(s8[5242880]{0:T(1024)(128)(4,1)} %bitcast.209), calls=%async_computation.10 | async-start | bytes 8388608
  179.3 12.7 %slice-start.4 = ((s8[5242880]{0:T(1024)(128)(4,1)}), s8[4194304]{0:T(1024)(128)(4,1)S(1)}, s32[]{:S(2)}) async-start(s8[5242880]{0:T(1024)(128)(4,1)} %bitcast.211), calls=%async_computation.12 | async-start | bytes 8388608
  186.6 5.4 slice-start.3
  186.6 5.4 slice-start.5
  192.0 37.8 %copy-start = (f32[64,2560]{1,0:T(8,128)S(1)}, f32[64,2560]{1,0:T(8,128)}, u32[]{:S(2)}) copy-start(f32[64,2560]{1,0:T(8,128)} %param.10) | copy-start | bytes 1966084
  195.6 114.4 %all-reduce.17.cloned.1.call-start = ((), (), s32[]{:S(2)}) async-start(), calls=%async_computation | async-start | bytes 655360 | tf_op jit(solution)/shard_map/psum | solution.py:39
  234.5 45.4 %copy-start.6 = (f32[2560]{0:T(1024)S(1)}, f32[2560]{0:T(1024)}, u32[]{:S(2)}) copy-start(f32[2560]{0:T(1024)} %get-tuple-element.8) | copy-start | bytes 30724
  279.8 155.1 %all-reduce.19.cloned.1.call-start = ((), (), s32[]{:S(2)}) async-start(), calls=%async_computation.1 | async-start | bytes 655360 | tf_op jit(solution)/shard_map/psum | solution.py:39
  361.3 44.7 %copy-start.5 = (f32[2560]{0:T(1024)S(1)}, f32[2560]{0:T(1024)}, u32[]{:S(2)}) copy-start(f32[2560]{0:T(1024)} %get-tuple-element.10) | copy-start | bytes 30724
  405.9 154.6 %all-reduce.21.cloned.1.call-start = ((), (), s32[]{:S(2)}) async-start(), calls=%async_computation.2 | async-start | bytes 655360 | tf_op jit(solution)/shard_map/psum | solution.py:39
  486.7 44.8 %copy-start.4 = (f32[2560]{0:T(1024)S(1)}, f32[2560]{0:T(1024)}, u32[]{:S(2)}) copy-start(f32[2560]{0:T(1024)} %get-tuple-element.11) | copy-start | bytes 30724
  531.4 154.0 %all-reduce.23.cloned.1.call-start = ((), (), s32[]{:S(2)}) async-start(), calls=%async_computation.3 | async-start | bytes 655360 | tf_op jit(solution)/shard_map/psum | solution.py:39
  611.8 44.8 %copy-start.3 = (f32[2560]{0:T(1024)S(1)}, f32[2560]{0:T(1024)}, u32[]{:S(2)}) copy-start(f32[2560]{0:T(1024)} %get-tuple-element.12) | copy-start | bytes 30724
  656.4 154.0 %all-reduce.25.cloned.1.call-start = ((), (), s32[]{:S(2)}) async-start(), calls=%async_computation.4 | async-start | bytes 655360 | tf_op jit(solution)/shard_map/psum | solution.py:39
  736.8 44.7 %copy-start.2 = (f32[2560]{0:T(1024)S(1)}, f32[2560]{0:T(1024)}, u32[]{:S(2)}) copy-start(f32[2560]{0:T(1024)} %get-tuple-element.13) | copy-start | bytes 30724
  781.4 154.2 %all-reduce.27.cloned.1.call-start = ((), (), s32[]{:S(2)}) async-start(), calls=%async_computation.5 | async-start | bytes 655360 | tf_op jit(solution)/shard_map/psum | solution.py:39
  861.8 44.9 %copy-start.1 = (f32[2560]{0:T(1024)S(1)}, f32[2560]{0:T(1024)}, u32[]{:S(2)}) copy-start(f32[2560]{0:T(1024)} %get-tuple-element.14) | copy-start | bytes 30724
  906.6 154.0 %all-reduce.29.cloned.1.call-start = ((), (), s32[]{:S(2)}) async-start(), calls=%async_computation.6 | async-start | bytes 655360 | tf_op jit(solution)/shard_map/psum | solution.py:39
Sparse Core Ops, SparseCore 0:
  195.7 33.3 all-reduce.30
  280.0 29.9 all-reduce.16
  406.0 28.8 all-reduce.18
  531.5 28.8 all-reduce.20
  656.5 28.8 all-reduce.22
  781.5 28.8 all-reduce.24
  906.7 28.8 all-reduce.26
  1031.7 28.8 all-reduce.28
